TPU v7x, 16 devices: a whole 2x2x2 slice. The times are simulated.
16 devices in a mesh: frag: 2 (over z), dev: 8 (over y, x, core).
Axes of the slice: x: 2, y: 2, z: 2, core: 2. Of those that a mesh axis runs over, the one named last changes fastest.
Arguments:
- a_ints: bfloat16 [208, 104, 104, 104], P(('frag', 'dev')), parts along dimension 0
- c_occ: bfloat16 [208, 32], P('frag'), parts along dimension 0
- c_vir: bfloat16 [208, 64], P('frag'), parts along dimension 0
- eps_occ: float32 [64], P('frag'), parts along dimension 0
- eps_vir: float32 [128], P('frag'), parts along dimension 0
Outputs:
- output: float32 [64, 32], P('frag', 'dev'), parts along dimension 0
There are 2 independent parts. A program takes and returns all parts, laid end to end along the dimension named above; each array names one.
All inputs are finite; a program needn't handle non-finite values.
Results may differ from a plain program's by a relative error of at most 0.001.
Values are sent between devices in bfloat16 or wider.
A program may use at most 1 GiB of HBM per device.

v0:
```python
import jax
import jax.numpy as jnp
from jax import lax
from jax.sharding import PartitionSpec as P, NamedSharding


def pair_energies(v_mo, eps_j, eps_occ, eps_vir):
    v_swap = jnp.swapaxes(v_mo, 1, 2)
    denominator = (eps_j[:, None, None, None] + eps_occ[None, None, None, :]
                   - eps_vir[None, :, None, None] - eps_vir[None, None, :, None])
    pair_ji = jnp.sum(v_mo * (2.0 * v_mo - v_swap) / denominator, axis=(1, 2))
    return pair_ji.T


def solution(mesh):
    group_size = mesh.shape["dev"]

    def per_device(a_ints, c_occ, c_vir, eps_occ, eps_vir):
        occ_dev = c_occ.shape[1] // group_size
        t_one = jnp.einsum("pqrs,rj->pqsj", a_ints, c_occ, preferred_element_type=jnp.float32).astype(jnp.bfloat16)
        half_mo = jnp.einsum("pqsj,sb->pqjb", t_one, c_vir, preferred_element_type=jnp.float32).astype(jnp.bfloat16)
        half_mo = lax.all_to_all(half_mo, "dev", 2, 0, tiled=True)
        g_mat = jnp.einsum("pqjb,qa->pjba", half_mo, c_vir, preferred_element_type=jnp.float32).astype(jnp.bfloat16)
        v_mo = jnp.einsum("pjba,pi->jbai", g_mat, c_occ, preferred_element_type=jnp.float32)
        eps_j = lax.dynamic_slice_in_dim(eps_occ, lax.axis_index("dev") * occ_dev, occ_dev)
        return pair_energies(v_mo, eps_j, eps_occ, eps_vir)

    return jax.shard_map(
        per_device,
        mesh=mesh,
        in_specs=(P(("frag", "dev")), P("frag"), P("frag"), P("frag"), P("frag")),
        out_specs=P("frag", "dev"),
        check_vma=False,
    )
```

profile of v0, /device:TPU:0, one launch (start us, length us, event | category | flops | bytes accessed | tf_op | source)
XLA Modules:
  0.0 156.3 jit_solution(11729022417371656039)
XLA Ops:
  0.0 0.0 copy-start
  0.0 13.2 %convolution_convert_fusion = bf16[13,104,104,32]{2,3,1,0:T(8,128)(2,1)S(1)} fusion(bf16[13,104,104,104]{3,2,1,0:T(8,128)(2,1)} %param.5, bf16[104,32]{0,1:T(8,128)(2,1)} %param.6), kind=kOutput, calls=%fused_computation.5 | convolution fusion | flops 940386304 | bytes 38252032 | tf_op jit(solution)/shard_map/pqrs,rj->pqsj/dot_general | solution.py:20
  13.2 0.0 copy-done
  13.3 15.1 %fusion.2 = bf16[13,104,32,64]{1,3,2,0:T(8,128)(2,1)} fusion(bf16[13,104,104,32]{2,3,1,0:T(8,128)(2,1)S(1)} %convolution_convert_fusion, bf16[104,64]{0,1:T(8,128)(2,1)S(1)} %copy-done), kind=kOutput, calls=%fused_computation.2 | convolution fusion | flops 578699264 | bytes 14550016 | tf_op jit(solution)/shard_map/pqsj,sb->pqjb/dot_general | solution.py:21
  28.3 7.5 %copy.14 = bf16[13,104,32,64]{1,3,0,2:T(8,128)(2,1)} copy(bf16[13,104,32,64]{1,3,2,0:T(8,128)(2,1)} %fusion.2) | data formatting | bytes 11075584 | tf_op jit(solution)/shard_map/convert_element_type | solution.py:21
  35.8 0.0 copy-start.3
  35.8 0.0 copy-start.2
  35.8 5.6 %all-to-all-start = ((bf16[13,104,32,64]{1,3,0,2:T(8,128)(2,1)}), bf16[13,104,32,64]{1,3,0,2:T(8,128)(2,1)}, u32[]{:S(2)}, u32[]{:S(2)}) async-start(bf16[13,104,32,64]{1,3,0,2:T(8,128)(2,1)} %copy.14), calls=%async_computation | async-start | bytes 13631488 | tf_op jit(solution)/shard_map/all_to_all | solution.py:22
  41.4 0.0 copy-done.3
  41.4 0.1 dynamic_slice.3
  41.5 0.1 broadcast_add_fusion
  41.6 0.0 copy-done.2
  41.6 0.1 broadcast_subtract_fusion
  41.7 77.2 %all-to-all-done = bf16[13,104,32,64]{1,3,0,2:T(8,128)(2,1)} async-done(((bf16[13,104,32,64]{1,3,0,2:T(8,128)(2,1)}), bf16[13,104,32,64]{1,3,0,2:T(8,128)(2,1)}, u32[]{:S(2)}, u32[]{:S(2)}) %all-to-all-start) | async-done | bytes 5537824 | tf_op jit(solution)/shard_map/all_to_all | solution.py:22
  118.8 0.0 copy-start.1
  118.9 8.2 %copy.16 = bf16[8,13,104,4,64]{2,4,3,1,0:T(8,128)(2,1)} copy(bf16[8,13,104,4,64]{2,4,1,3,0:T(8,128)(2,1)} %bitcast.6) | data formatting | bytes 11075584 | tf_op jit(solution)/shard_map/all_to_all | solution.py:22
  127.1 0.0 copy-done.1
  127.1 17.7 %fusion.9 = f32[4,64,64,32]{2,3,1,0:T(8,128)} fusion(bf16[104,104,4,64]{1,3,2,0:T(8,128)(2,1)} %bitcast.29, bf16[104,64]{0,1:T(8,128)(2,1)S(1)} %copy-done, bf16[104,32]{0,1:T(8,128)(2,1)S(1)} %copy-done.1), kind=kOutput, calls=%fused_computation.9 | convolution fusion | flops 465174528 | bytes 7654912 | tf_op jit(solution)/shard_map/pjba,pi->jbai/dot_general | solution.py:24
  144.7 6.8 %copy.18 = f32[4,64,64,32]{1,3,2,0:T(8,128)} copy(f32[4,64,64,32]{2,3,1,0:T(8,128)} %fusion.9) | data formatting | bytes 4194304 | tf_op jit(solution)/shard_map/pjba,pi->jbai/dot_general | solution.py:24
  151.5 4.8 %fusion.11 = f32[4,32]{1,0:T(4,128)} fusion(f32[4,64,64,32]{2,3,1,0:T(8,128)} %fusion.9, f32[4,64,64,32]{1,3,2,0:T(8,128)} %copy.18, f32[64]{0:T(128)S(1)} %copy-done.2, f32[4,64,32]{2,1,0:T(8,128)S(1)} %broadcast_subtract_fusion), kind=kLoop, calls=%fused_computation.11 | loop fusion | flops 3145600 | bytes 4227840 | tf_op jit(solution)/shard_map/reduce_sum | solution.py:11
Async XLA Ops:
  0.0 13.3 %copy-start = (bf16[104,64]{0,1:T(8,128)(2,1)S(1)}, bf16[104,64]{0,1:T(8,128)(2,1)}, u32[]{:S(2)}) copy-start(bf16[104,64]{0,1:T(8,128)(2,1)} %param.7) | copy-start | bytes 39940
  35.8 5.6 %copy-start.3 = (f32[32]{0:T(128)S(1)}, f32[32]{0:T(128)}, u32[]{:S(2)}) copy-start(f32[32]{0:T(128)} %param.8) | copy-start | bytes 388
  35.8 5.8 %copy-start.2 = (f32[64]{0:T(128)S(1)}, f32[64]{0:T(128)}, u32[]{:S(2)}) copy-start(f32[64]{0:T(128)} %param.9) | copy-start | bytes 772
  35.8 83.0 %all-to-all-start = ((bf16[13,104,32,64]{1,3,0,2:T(8,128)(2,1)}), bf16[13,104,32,64]{1,3,0,2:T(8,128)(2,1)}, u32[]{:S(2)}, u32[]{:S(2)}) async-start(bf16[13,104,32,64]{1,3,0,2:T(8,128)(2,1)} %copy.14), calls=%async_computation | async-start | bytes 13631488 | tf_op jit(solution)/shard_map/all_to_all | solution.py:22
  118.8 8.2 %copy-start.1 = (bf16[104,32]{0,1:T(8,128)(2,1)S(1)}, bf16[104,32]{0,1:T(8,128)(2,1)}, u32[]{:S(2)}) copy-start(bf16[104,32]{0,1:T(8,128)(2,1)} %param.6) | copy-start | bytes 19972
where the time goes:
time: 157 us; the launch traced here: 156 us
  waiting for transfers between devices  77.2 us (49%)
  matrix products  46 us (29%)
  local copies, waits for them, and re-layouts  22.6 us (14%)
  starting transfers between devices  5.59 us (4%)
  other arithmetic  4.9 us (3%)
    all_to_all x1, waiting for transfers between devices, per_device(): half_mo = lax.all_to_all(half_mo, 'dev', 2, 0, tiled=True)  77.2 us
    dot_general x1, matrix products, per_device(): jnp.einsum('pjba,pi->jbai', g_mat, c_occ, preferred_element_type=jnp.floa...  17.7 us
    dot_general x1, matrix products, per_device(): jnp.einsum('pqsj,sb->pqjb', t_one, c_vir, preferred_element_type=jnp.floa...  15.1 us
    dot_general x1, matrix products, per_device(): jnp.einsum('pqrs,rj->pqsj', a_ints, c_occ, preferred_element_type=jnp.flo...  13.2 us
    all_to_all x1, local copies, waits for them, and re-layouts, per_device(): half_mo = lax.all_to_all(half_mo, 'dev', 2, 0, tiled=True)  8.2 us
    convert_element_type x1, local copies, waits for them, and re-layouts, per_device(): jnp.einsum('pqsj,sb->pqjb', t_one, c_vir, preferred_element_type=jnp.floa...  7.48 us
    dot_general x1, local copies, waits for them, and re-layouts, per_device(): jnp.einsum('pjba,pi->jbai', g_mat, c_occ, preferred_element_type=jnp.floa...  6.78 us
    all_to_all x1, starting transfers between devices, per_device(): half_mo = lax.all_to_all(half_mo, 'dev', 2, 0, tiled=True)  5.59 us
  transfers between devices with their start and end apart: 1, of which 1 were waited for; matrix products, arithmetic and copies ran while one was open for 0% of the time, Pallas kernels for 0%

commit v1 on v0

v1 whole, which is shorter than its diff:
```python
import functools

import jax
import jax.numpy as jnp
from jax import lax
from jax.experimental import pallas as pl
from jax.experimental.pallas import tpu as pltpu
from jax.sharding import PartitionSpec as P


MESH = pl.DeviceIdType.MESH
SUB = 16
F32 = jnp.float32
BF16 = jnp.bfloat16


def iota(shape, dim):
    return lax.broadcasted_iota(jnp.int32, shape, dim)


def ones_where(cond):
    return jnp.where(cond, 1.0, 0.0).astype(BF16)


def dot(a, b):
    return jnp.dot(a, b, preferred_element_type=F32)


def dot_t(a, b):
    return lax.dot_general(a, b, (((1,), (1,)), ((), ())), preferred_element_type=F32)


def kernel(n, o, v, group, rows, a_hbm, cot_ref, cvt_ref, eo_ref, ev_ref, e_ref,
           abuf, l1, w2, l3, l4, tp, hs, gsend, recv, vacc, rden, esum, a_sem, send_sem, recv_sem):
    me = lax.axis_index("dev")
    slots = abuf.shape[0]
    block = 2 * v

    def load(p, slot):
        return pltpu.make_async_copy(a_hbm.at[p], abuf.at[slot], a_sem.at[slot])

    for p in range(slots):
        load(p, p).start()

    def peer(k):
        core, x, y = lax.rem(me, 2), lax.rem(me // 2, 2), me // 4
        return 4 * lax.rem(y + k // 4, 2) + 2 * lax.rem(x + k // 2 % 2, 2) + lax.rem(core + k % 2, 2)

    barrier = pltpu.get_barrier_semaphore()
    for k in range(1, group):
        pl.semaphore_signal(barrier, inc=1, device_id={"dev": peer(k)}, device_id_type=MESH)

    row = iota((64, o), 0)
    perm = ones_where(2 * (row % SUB) + row // SUB % 2 == iota((64, o), 1))
    cotp = dot(perm, cot_ref[...]).astype(BF16)
    spread = ones_where(iota((n, 2 * n), 1) % n == iota((n, 2 * n), 0))
    same = iota((64, 2 * n), 0) // 32 == iota((64, 2 * n), 1) // n
    l1[...] = jnp.where(same, dot(cotp, spread), 0.0).astype(BF16)
    spread = ones_where(iota((256, n), 0) % 128 == iota((256, n), 1))
    same = iota((256, 2 * v), 0) // 128 == iota((256, 2 * v), 1) // v
    cvt2 = jnp.concatenate([cvt_ref[...], cvt_ref[...]], axis=0)
    w2[...] = jnp.where(same, dot_t(spread, cvt2), 0.0).astype(BF16)
    spread = ones_where(iota((n, SUB * n), 1) // SUB == iota((n, SUB * n), 0))
    cvrep = dot(cvt_ref[...], spread)
    for j in range(SUB):
        l3[j * v:(j + 1) * v, :] = jnp.where(iota((v, SUB * n), 1) % SUB == j, cvrep, 0.0).astype(BF16)

    def send(p, k):
        return pltpu.make_async_remote_copy(
            src_ref=gsend.at[p, pl.ds(pl.multiple_of(peer(k) * block, block), block)],
            dst_ref=recv.at[p, me],
            send_sem=send_sem,
            recv_sem=recv_sem.at[p],
            device_id={"dev": peer(k)},
            device_id_type=MESH,
        )

    pad = jnp.zeros((2 * n, 128 - n), BF16)

    def make_g(p):
        slot = lax.rem(p, slots)
        load(p, slot).wait()

        def tile(t, carry):
            base = pl.multiple_of(t * 4 * n, SUB)
            left = abuf[slot, pl.ds(base, 2 * n), :]
            right = abuf[slot, pl.ds(base + 2 * n, 2 * n), :]
            out = dot(l1[...], jnp.concatenate([left, pad, right, pad], axis=1)).astype(BF16)
            for qn in range(2):
                for qk in range(2):
                    to = pl.ds(pl.multiple_of(t * 64 + (2 * qn + qk) * SUB, SUB), SUB)
                    for jh in range(2):
                        at = qk * 32 + jh * SUB
                        tp[to, jh * 128:(jh + 1) * 128] = out[at:at + SUB, qn * 128:(qn + 1) * 128]
            return carry

        lax.fori_loop(0, n // 4, tile, 0, unroll=n // 4)
        hs[...] = dot(tp[...], w2[...]).astype(BF16)
        gsend[p] = dot(l3[...], hs[...]).astype(BF16)

        @pl.when(p + slots < rows)
        def _():
            load(p + slots, slot).start()

    make_g(0)
    pl.semaphore_wait(barrier, group - 1)

    def hand_out(p):
        for k in (6, 7, 4, 5, 2, 3, 1):
            send(p, k).start()
        recv[p, me] = gsend[p, pl.ds(pl.multiple_of(me * block, block), block), :]

    hand_out(0)

    @pl.loop(1, rows)
    def _(p):
        make_g(p)
        hand_out(p)

    lane = iota((n, SUB * n), 1) // SUB
    spread = ones_where(lane % group * rows + lane // group == iota((n, SUB * n), 0))
    corep = dot(cot_ref[...], spread).astype(BF16)
    split = ones_where(iota((SUB * o, o), 0) // SUB == iota((SUB * o, o), 1))
    diag = iota((SUB * o, SUB * n), 0) % SUB == iota((SUB * o, SUB * n), 1) % SUB
    l4[...] = jnp.where(diag, dot(split, corep), 0.0).astype(BF16)

    ev = ev_ref[...]
    ev_b = jnp.concatenate([ev, ev], axis=1)
    ev_a = jnp.transpose(jnp.broadcast_to(ev_b, (128, 128)))
    at = me * (o // group)
    first = iota((128, 128), 0) < v
    even = iota((128, 128), 1) < v
    eo_j = jnp.where(first, jnp.where(even, eo_ref[at], eo_ref[at + 1]),
                     jnp.where(even, eo_ref[at + 2], eo_ref[at + 3]))

    @pl.loop(0, o)
    def _(i):
        rden[i] = 1.0 / (eo_j + eo_ref[i] - ev_a - ev_b)

    def arrived(p):
        pltpu.make_async_remote_copy(
            src_ref=recv.at[p, pl.ds(0, group - 1)],
            dst_ref=recv.at[p, pl.ds(0, group - 1)],
            send_sem=send_sem,
            recv_sem=recv_sem.at[p],
            device_id={"dev": peer(1)},
            device_id_type=MESH,
        ).wait_recv()

    def add(lo, hi):
        for p in range(lo, hi):
            arrived(p)
        depth = (hi - lo) * group * SUB
        for g in range(v // SUB):
            parts = [recv[lo:hi, :, x * v + g * SUB:x * v + (g + 1) * SUB, :].reshape(depth, 128) for x in range(2)]
            part = dot(l4[:, lo * group * SUB:hi * group * SUB], jnp.concatenate(parts, axis=1))
            vacc[g] = part if lo == 0 else vacc[g] + part

    add(0, 8)
    add(8, 12)
    add(12, rows)

    @pl.loop(0, o, unroll=4)
    def _(i):
        at = pl.ds(pl.multiple_of(i * SUB, SUB), SUB)
        halves = [jnp.concatenate([vacc[g, at, x * 128:(x + 1) * 128] for g in range(v // SUB)], axis=0)
                  for x in range(2)]
        mat = jnp.concatenate(halves, axis=0)
        mat_t = jnp.transpose(mat)
        turned = pltpu.roll(jnp.concatenate([mat_t[v:], mat_t[:v]], axis=0), v, 1)
        swap = jnp.where(first == even, mat_t, turned)
        term = mat * (2.0 * mat - swap) * rden[i]
        for x in range(2):
            esum[x, i] = jnp.sum(term[x * v:(x + 1) * v].reshape(v // 8, 8, 128), axis=0)

    lane = iota((o, 128), 1)
    out = jnp.zeros((o, 128), F32)
    for x in range(2):
        both = jnp.sum(esum[x], axis=1)
        for jh in range(2):
            total = jnp.sum(jnp.where(lane // v == jh, both, 0.0), axis=1, keepdims=True)
            out = jnp.where(lane == 2 * x + jh, total, out)
    e_ref[...] = out[:, :o // group]

    pltpu.make_async_remote_copy(
        src_ref=gsend.at[:, pl.ds(0, (group - 1) * block)],
        dst_ref=gsend.at[:, pl.ds(0, (group - 1) * block)],
        send_sem=send_sem,
        recv_sem=recv_sem.at[0],
        device_id={"dev": peer(1)},
        device_id_type=MESH,
    ).wait_send()


def solution(mesh):
    group = mesh.shape["dev"]

    def per_device(a_ints, c_occ, c_vir, eps_occ, eps_vir):
        rows, n = a_ints.shape[:2]
        o, v = c_occ.shape[1], c_vir.shape[1]
        vmem = pl.BlockSpec(memory_space=pltpu.VMEM)
        return pl.pallas_call(
            functools.partial(kernel, n, o, v, group, rows),
            out_shape=jax.ShapeDtypeStruct((o, o // group), F32),
            in_specs=[pl.BlockSpec(memory_space=pl.ANY), vmem, vmem,
                      pl.BlockSpec(memory_space=pltpu.SMEM), vmem],
            out_specs=vmem,
            scratch_shapes=[
                pltpu.VMEM((3, n * n, n), BF16),
                pltpu.VMEM((64, 2 * n), BF16),
                pltpu.VMEM((256, 128), BF16),
                pltpu.VMEM((SUB * v, SUB * n), BF16),
                pltpu.VMEM((SUB * o, SUB * n), BF16),
                pltpu.VMEM((SUB * n, 256), BF16),
                pltpu.VMEM((SUB * n, 128), BF16),
                pltpu.VMEM((rows, SUB * v, 128), BF16),
                pltpu.VMEM((rows, group, 2 * v, 128), BF16),
                pltpu.VMEM((v // SUB, SUB * o, 256), F32),
                pltpu.VMEM((o, 128, 128), F32),
                pltpu.VMEM((2, o, 8, 128), F32),
                pltpu.SemaphoreType.DMA((3,)),
                pltpu.SemaphoreType.DMA,
                pltpu.SemaphoreType.DMA((rows,)),
            ],
            compiler_params=pltpu.CompilerParams(
                collective_id=0, has_side_effects=True, vmem_limit_bytes=60 * 2**20),
        )(a_ints.reshape(rows, n * n, n), c_occ.T, c_vir.T, eps_occ, eps_vir.reshape(1, v))

    return jax.shard_map(
        per_device,
        mesh=mesh,
        in_specs=(P(("frag", "dev")), P("frag"), P("frag"), P("frag"), P("frag")),
        out_specs=P("frag", "dev"),
        check_vma=False,
    )
```

time: 157 us -> 49.8 us (0.32)
  waiting for transfers between devices: 77.2 us -> 0 us
  Pallas kernels: 0 us -> 48.1 us
  matrix products: 46 us -> 0 us
  local copies, waits for them, and re-layouts: 22.6 us -> 1.37 us
  starting transfers between devices: 5.59 us -> 0 us
  other arithmetic: 4.9 us -> 0 us
    all_to_all x1 -> x0, waiting for transfers between devices: 77.2 us -> none  [per_device(): half_mo = lax.all_to_all(half_mo, 'dev', 2, 0, tiled=True)]
    pallas_call x0 -> x1, Pallas kernels: none -> 48.1 us  [per_device(): pl.pallas_call(functools.partial(kernel, n, o, v, group, rows), out_shape...]
    dot_general x3 -> x0, matrix products: 46 us -> none  [the longest x1 17.7 us: per_device(): jnp.einsum('pjba,pi->jbai', g_mat, c_occ, preferred_element_type=jnp.floa...]
    all_to_all x1 -> x0, local copies, waits for them, and re-layouts: 8.2 us -> none  [per_device(): half_mo = lax.all_to_all(half_mo, 'dev', 2, 0, tiled=True)]
    convert_element_type x1 -> x0, local copies, waits for them, and re-layouts: 7.48 us -> none  [per_device(): jnp.einsum('pqsj,sb->pqjb', t_one, c_vir, preferred_element_type=jnp.floa...]
    dot_general x1 -> x0, local copies, waits for them, and re-layouts: 6.78 us -> none  [per_device(): jnp.einsum('pjba,pi->jbai', g_mat, c_occ, preferred_element_type=jnp.floa...]
    all_to_all x1 -> x0, starting transfers between devices: 5.59 us -> none  [per_device(): half_mo = lax.all_to_all(half_mo, 'dev', 2, 0, tiled=True)]
    reduce_sum x1 -> x0, other arithmetic: 4.75 us -> none  [pair_energies(): pair_ji = jnp.sum(v_mo * (2.0 * v_mo - v_swap) / denominator, axis=(1, 2))]
  transfers between devices with their start and end apart: 1 -> 0, of which waited for: 1 -> 0; matrix products, arithmetic and copies ran while one was open for 0% -> 0% of each run, Pallas kernels for 0% -> 0%
where the time goes in v1:
time: 49.8 us; the launch traced here: 49.5 us
  Pallas kernels  48.1 us (97%)
  local copies, waits for them, and re-layouts  1.37 us (3%)
    pallas_call x1, Pallas kernels, per_device(): pl.pallas_call(functools.partial(kernel, n, o, v, group, rows), out_shape...  48.1 us
    pallas_call x1, local copies, waits for them, and re-layouts, per_device(): pl.pallas_call(functools.partial(kernel, n, o, v, group, rows), out_shape...  1.37 us

profile of v1, /device:TPU:0, one launch (start us, length us, event | category | flops | bytes accessed | tf_op | source)
XLA Modules:
  0.0 49.5 jit_solution(15655715215637052220)
XLA Ops:
  0.0 48.1 %shard_map.55 = f32[32,4]{1,0:T(8,128)} custom-call(bf16[13,10816,104]{2,1,0:T(8,128)(2,1)} %bitcast.4, bf16[32,104]{1,0:T(8,128)(2,1)} %bitcast.6, bf16[64,104]{1,0:T(8,128)(2,1)} %bitcast.5, f32[32]{0:T(128)} %eo_ref.1, f32[1,64]{1,0:T(1,128)} %bitcast.7), custom_call_target="tpu_custom_call" | custom-call | tf_op jit(solution)/shard_map/pallas_call | solution.py:202
  48.1 1.4 %copy.6 = f32[32,4]{0,1:T(4,128)} copy(f32[32,4]{1,0:T(8,128)} %shard_map.55) | data formatting | bytes 1024 | tf_op jit(solution)/shard_map/pallas_call | solution.py:202

commit v2 on v1

v2 whole, which is shorter than its diff:
```python
import functools

import jax
import jax.numpy as jnp
from jax import lax
from jax.experimental import pallas as pl
from jax.experimental.pallas import tpu as pltpu
from jax.sharding import PartitionSpec as P


MESH = pl.DeviceIdType.MESH
SUB = 16
LATE = 5
FAR, NEAR = (6, 7, 4, 5), (2, 3, 1)
F32 = jnp.float32
BF16 = jnp.bfloat16


def iota(shape, dim):
    return lax.broadcasted_iota(jnp.int32, shape, dim)


def ones_where(cond):
    return jnp.where(cond, 1.0, 0.0).astype(BF16)


def dot(a, b):
    return jnp.dot(a, b, preferred_element_type=F32)


def dot_t(a, b):
    return lax.dot_general(a, b, (((1,), (1,)), ((), ())), preferred_element_type=F32)


def kernel(n, o, v, group, rows, a_hbm, cot_hbm, cvt_hbm, eo_hbm, ev_hbm, e_ref,
           abuf, cot, cvt, eo, ev_ref, l1, w2, l3, l4, tp, hs, gsend, recv, vacc, rden, esum,
           a_sem, in_sem, send_sem, recv_sem):
    me = lax.axis_index("dev")
    slots = abuf.shape[0]
    tiles = n // 4
    cuts = [tiles * c // 26 for c in (0, 9, 17, 23, 26)]

    def load(p, slot):
        return pltpu.make_async_copy(a_hbm.at[p], abuf.at[slot], a_sem.at[slot])

    def load_first(c):
        at = pl.ds(cuts[c] * 4 * n, (cuts[c + 1] - cuts[c]) * 4 * n)
        return pltpu.make_async_copy(a_hbm.at[0, at], abuf.at[0, at], in_sem.at[4 + c])

    small = [pltpu.make_async_copy(src, dst, in_sem.at[k]) for k, (src, dst) in enumerate(
        [(cot_hbm, cot), (cvt_hbm, cvt), (eo_hbm, eo), (ev_hbm, ev_ref)])]
    for copy in small:
        copy.start()
    for c in range(4):
        load_first(c).start()

    def peer(k):
        core, x, y = lax.rem(me, 2), lax.rem(me // 2, 2), me // 4
        return 4 * lax.rem(y + k // 4, 2) + 2 * lax.rem(x + k // 2 % 2, 2) + lax.rem(core + k % 2, 2)

    barrier = pltpu.get_barrier_semaphore()
    for k in range(1, group):
        pl.semaphore_signal(barrier, inc=1, device_id={"dev": peer(k)}, device_id_type=MESH)
    for copy in small:
        copy.wait()

    row = iota((64, o), 0)
    perm = ones_where(2 * (row % SUB) + row // SUB % 2 == iota((64, o), 1))
    cotp = dot(perm, cot[...]).astype(BF16)
    spread = ones_where(iota((n, 2 * n), 1) % n == iota((n, 2 * n), 0))
    same = iota((64, 2 * n), 0) // 32 == iota((64, 2 * n), 1) // n
    l1[...] = jnp.where(same, dot(cotp, spread), 0.0).astype(BF16)
    spread = ones_where(iota((256, n), 0) % 128 == iota((256, n), 1))
    same = iota((256, 2 * v), 0) // 128 == iota((256, 2 * v), 1) // v
    cvt2 = jnp.concatenate([cvt[...], cvt[...]], axis=0)
    w2[...] = jnp.where(same, dot_t(spread, cvt2), 0.0).astype(BF16)
    spread = ones_where(iota((n, SUB * n), 1) // SUB == iota((n, SUB * n), 0))
    cvrep = dot(cvt[...], spread).astype(BF16)
    for j in range(SUB):
        pick = (iota((v, SUB * n), 1) % SUB == j)
        l3[j * v:(j + 1) * v, :] = jnp.where(pick, cvrep, jnp.zeros_like(cvrep))

    def send(p, x, k):
        return pltpu.make_async_remote_copy(
            src_ref=gsend.at[p, pl.ds(pl.multiple_of((2 * peer(k) + x) * v, v), v)],
            dst_ref=recv.at[x, p, me],
            send_sem=send_sem,
            recv_sem=recv_sem.at[x, p],
            device_id={"dev": peer(k)},
            device_id_type=MESH,
        )

    pad = jnp.zeros((2 * n, 128 - n), BF16)

    def tile(slot, t):
        base = t * 4 * n if isinstance(t, int) else pl.multiple_of(t * 4 * n, SUB)
        left = abuf[slot, pl.ds(base, 2 * n), :]
        right = abuf[slot, pl.ds(base + 2 * n, 2 * n), :]
        out = dot(l1[...], jnp.concatenate([left, pad, right, pad], axis=1)).astype(BF16)
        for qn in range(2):
            for qk in range(2):
                to = t * 64 + (2 * qn + qk) * SUB
                to = pl.ds(to if isinstance(t, int) else pl.multiple_of(to, SUB), SUB)
                for jh in range(2):
                    at = qk * 32 + jh * SUB
                    tp[to, jh * 128:(jh + 1) * 128] = out[at:at + SUB, qn * 128:(qn + 1) * 128]

    def finish(p, chip, chips):
        at = pl.ds(pl.multiple_of(chip * 4 * v, 4 * v), chips * 4 * v)
        gsend[p, at, :] = dot(l3[at, :], hs[...]).astype(BF16)

    def hand_out(p, ks, xs):
        for x in xs:
            for k in ks:
                send(p, x, k).start()

    def keep(p):
        for x in range(2):
            recv[x, p, me] = gsend[p, pl.ds(pl.multiple_of((2 * me + x) * v, v), v), :]

    for c in range(4):
        load_first(c).wait()
        if c == 2:
            for p in range(1, slots):
                load(p, p).start()
        for t in range(cuts[c], cuts[c + 1]):
            tile(0, t)
        at = slice(cuts[c] * 64, cuts[c + 1] * 64)
        hs[at, :] = dot(tp[at, :], w2[...]).astype(BF16)
    load(slots, 0).start()
    finish(0, peer(6) // 2, 1)
    pl.semaphore_wait(barrier, group - 1)
    hand_out(0, (6, 7), (0, 1))
    finish(0, peer(4) // 2, 1)
    hand_out(0, (4, 5), (0, 1))
    finish(0, me // 4 * 2, 2)
    hand_out(0, NEAR, (0, 1))
    keep(0)

    @pl.loop(1, rows)
    def _(p):
        slot = lax.rem(p, slots)
        load(p, slot).wait()
        lax.fori_loop(0, tiles, lambda t, _: tile(slot, t), None, unroll=tiles)

        @pl.when(p + slots < rows)
        def _():
            load(p + slots, slot).start()

        hs[...] = dot(tp[...], w2[...]).astype(BF16)
        gsend[p] = dot(l3[...], hs[...]).astype(BF16)
        hand_out(p, FAR + NEAR, (0,))

        @pl.when(p < rows - LATE)
        def _():
            hand_out(p, FAR + NEAR, (1,))

        keep(p)

    @pl.loop(rows - LATE, rows)
    def _(p):
        hand_out(p, FAR + NEAR, (1,))

    lane = iota((n, SUB * n), 1) // SUB
    spread = ones_where(lane % group * rows + lane // group == iota((n, SUB * n), 0))
    corep = dot(cot[...], spread).astype(BF16)
    split = ones_where(iota((SUB * o, o), 0) // SUB == iota((SUB * o, o), 1))
    diag = iota((SUB * o, SUB * n), 0) % SUB == iota((SUB * o, SUB * n), 1) % SUB
    l4[...] = jnp.where(diag, dot(split, corep), 0.0).astype(BF16)

    ev = ev_ref[...]
    ev_b = jnp.concatenate([ev, ev], axis=1)
    ev_a = jnp.transpose(jnp.broadcast_to(ev_b, (128, 128)))
    first = iota((128, 128), 0) < v
    even = iota((128, 128), 1) < v

    @pl.loop(0, o // 2)
    def _(i):
        eo_i = jnp.where(first, eo[2 * i], eo[2 * i + 1])
        for x in range(2):
            at = me * (o // group) + 2 * x
            eo_j = jnp.where(even, eo[at], eo[at + 1])
            rden[x, i] = 1.0 / (eo_i + eo_j - ev_a - ev_b)

    def arrived(x, p):
        pltpu.make_async_remote_copy(
            src_ref=recv.at[x, p, pl.ds(0, group - 1)],
            dst_ref=recv.at[x, p, pl.ds(0, group - 1)],
            send_sem=send_sem,
            recv_sem=recv_sem.at[x, p],
            device_id={"dev": peer(1)},
            device_id_type=MESH,
        ).wait_recv()

    def add(x, lo, hi):
        for p in range(lo, hi):
            arrived(x, p)
        depth = (hi - lo) * group * SUB
        for h in range(2):
            parts = [recv[x, lo:hi, :, (2 * h + g) * SUB:(2 * h + g + 1) * SUB, :].reshape(depth, 128) for g in range(2)]
            part = dot(l4[:, lo * group * SUB:hi * group * SUB], jnp.concatenate(parts, axis=1))
            vacc[x, h] = part if lo == 0 else vacc[x, h] + part

    def energies(x):
        @pl.loop(0, o // 2, unroll=o // 2)
        def _(i):
            mats = []
            for i2 in range(2):
                at = pl.ds(pl.multiple_of((2 * i + i2) * SUB, SUB), SUB)
                mats += [vacc[x, g // 2, at, g % 2 * 128:(g % 2 + 1) * 128] for g in range(v // SUB)]
            mat = jnp.concatenate(mats, axis=0)
            mat_t = jnp.transpose(mat)
            turned = pltpu.roll(jnp.concatenate([mat_t[v:], mat_t[:v]], axis=0), v, 1)
            swap = jnp.where(first == even, mat_t, turned)
            term = mat * (2.0 * mat - swap) * rden[x, i]
            for i2 in range(2):
                esum[x, 2 * i + i2] = jnp.sum(term[i2 * v:(i2 + 1) * v].reshape(v // 8, 8, 128), axis=0)

    lane = iota((o, 128), 1)
    out = jnp.zeros((o, 128), F32)
    for x in range(2):
        add(x, 0, 8)
        add(x, 8, 12)
        add(x, 12, rows)
        energies(x)
        both = jnp.sum(esum[x], axis=1)
        for jh in range(2):
            total = jnp.sum(jnp.where(lane // v == jh, both, 0.0), axis=1, keepdims=True)
            out = jnp.where(lane == 2 * x + jh, total, out)
    e_ref[...] = jnp.transpose(out)[:o // group, :]

    pltpu.make_async_remote_copy(
        src_ref=gsend.at[:, pl.ds(0, (group - 1) * 2 * v)],
        dst_ref=gsend.at[:, pl.ds(0, (group - 1) * 2 * v)],
        send_sem=send_sem,
        recv_sem=recv_sem.at[0, 0],
        device_id={"dev": peer(1)},
        device_id_type=MESH,
    ).wait_send()


def solution(mesh):
    group = mesh.shape["dev"]

    def per_device(a_ints, c_occ, c_vir, eps_occ, eps_vir):
        rows, n = a_ints.shape[:2]
        o, v = c_occ.shape[1], c_vir.shape[1]
        hbm = pl.BlockSpec(memory_space=pltpu.HBM)
        return pl.pallas_call(
            functools.partial(kernel, n, o, v, group, rows),
            out_shape=jax.ShapeDtypeStruct((o // group, o), F32),
            in_specs=[hbm] * 5,
            out_specs=pl.BlockSpec(memory_space=pltpu.VMEM),
            scratch_shapes=[
                pltpu.VMEM((3, n * n, n), BF16),
                pltpu.VMEM((o, n), BF16),
                pltpu.VMEM((v, n), BF16),
                pltpu.SMEM((o,), F32),
                pltpu.VMEM((1, v), F32),
                pltpu.VMEM((64, 2 * n), BF16),
                pltpu.VMEM((256, 128), BF16),
                pltpu.VMEM((SUB * v, SUB * n), BF16),
                pltpu.VMEM((SUB * o, SUB * n), BF16),
                pltpu.VMEM((SUB * n, 256), BF16),
                pltpu.VMEM((SUB * n, 128), BF16),
                pltpu.VMEM((rows, SUB * v, 128), BF16),
                pltpu.VMEM((2, rows, group, v, 128), BF16),
                pltpu.VMEM((2, 2, SUB * o, 256), F32),
                pltpu.VMEM((2, o // 2, 128, 128), F32),
                pltpu.VMEM((2, o, 8, 128), F32),
                pltpu.SemaphoreType.DMA((3,)),
                pltpu.SemaphoreType.DMA((8,)),
                pltpu.SemaphoreType.DMA,
                pltpu.SemaphoreType.DMA((2, rows)),
            ],
            compiler_params=pltpu.CompilerParams(
                collective_id=0, has_side_effects=True, vmem_limit_bytes=60 * 2**20),
        )(a_ints.reshape(rows, n * n, n), c_occ.T, c_vir.T, eps_occ, eps_vir.reshape(1, v)).T

    return jax.shard_map(
        per_device,
        mesh=mesh,
        in_specs=(P(("frag", "dev")), P("frag"), P("frag"), P("frag"), P("frag")),
        out_specs=P("frag", "dev"),
        check_vma=False,
    )
```

time: 49.8 us -> 48 us (0.964)
  Pallas kernels: 48.1 us -> 46.5 us
    pallas_call x1, Pallas kernels: 48.1 us -> 46.5 us  [per_device(): pl.pallas_call(functools.partial(kernel, n, o, v, group, rows), out_shape...]
    pallas_call x1 -> x0, local copies, waits for them, and re-layouts: 1.37 us -> none  [per_device(): pl.pallas_call(functools.partial(kernel, n, o, v, group, rows), out_shape...]
    unnamed x0 -> x1, local copies, waits for them, and re-layouts: none -> 1.26 us
where the time goes in v2:
time: 48 us; the launch traced here: 47.8 us
  Pallas kernels  46.5 us (97%)
  local copies, waits for them, and re-layouts  1.26 us (3%)
    pallas_call x1, Pallas kernels, per_device(): pl.pallas_call(functools.partial(kernel, n, o, v, group, rows), out_shape...  46.5 us
    unnamed x1, local copies, waits for them, and re-layouts  1.26 us

profile of v2, /device:TPU:0, one launch (start us, length us, event | category | flops | bytes accessed | tf_op | source)
XLA Modules:
  0.0 47.8 jit_solution(15255776850547267254)
XLA Ops:
  0.0 46.5 %shard_map.55 = f32[4,32]{1,0:T(4,128)} custom-call(bf16[13,10816,104]{2,1,0:T(8,128)(2,1)} %bitcast.5, bf16[32,104]{1,0:T(8,128)(2,1)} %bitcast.7, bf16[64,104]{1,0:T(8,128)(2,1)} %bitcast.6, f32[32]{0:T(128)} %eo_hbm.1, f32[1,64]{1,0:T(1,128)} %bitcast.9), custom_call_target="tpu_custom_call" | custom-call | tf_op jit(solution)/shard_map/pallas_call | solution.py:249
  46.5 1.3 %copy.7 = f32[32,4]{0,1:T(4,128)} copy(f32[32,4]{0,1:T(4,128)} %bitcast.8) | data formatting | bytes 1024

commit v3 on v2

--- a/solution.py
+++ b/solution.py
@@ -248,7 +248,7 @@
         hbm = pl.BlockSpec(memory_space=pltpu.HBM)
         return pl.pallas_call(
             functools.partial(kernel, n, o, v, group, rows),
-            out_shape=jax.ShapeDtypeStruct((o // group, o), F32),
+            out_shape=pltpu.VMEM((o // group, o), F32),
             in_specs=[hbm] * 5,
             out_specs=pl.BlockSpec(memory_space=pltpu.VMEM),
             scratch_shapes=[
@@ -274,8 +274,9 @@
                 pltpu.SemaphoreType.DMA((2, rows)),
             ],
             compiler_params=pltpu.CompilerParams(
-                collective_id=0, has_side_effects=True, vmem_limit_bytes=60 * 2**20),
-        )(a_ints.reshape(rows, n * n, n), c_occ.T, c_vir.T, eps_occ, eps_vir.reshape(1, v)).T
+                collective_id=0, has_side_effects=True, vmem_limit_bytes=40 * 2**20),
+        )(*(pltpu.with_memory_space_constraint(x, pltpu.HBM)
+            for x in (a_ints.reshape(rows, n * n, n), c_occ.T, c_vir.T, eps_occ, eps_vir.reshape(1, v)))).T
 
     return jax.shard_map(
         per_device,

time: 48 us -> 46.7 us (0.973)
  local copies, waits for them, and re-layouts: 1.26 us -> 0.58 us
  Pallas kernels: 46.5 us -> 45.9 us
    unnamed x1, local copies, waits for them, and re-layouts: 1.26 us -> 0.58 us
    pallas_call x1, Pallas kernels: 46.5 us -> 45.9 us  [per_device(): pl.pallas_call(functools.partial(kernel, n, o, v, group, rows), out_shape...]
where the time goes in v3:
time: 46.7 us; the launch traced here: 46.5 us
  Pallas kernels  45.9 us (98%)
  local copies, waits for them, and re-layouts  0.58 us (1%)
    pallas_call x1, Pallas kernels, per_device(): pl.pallas_call(functools.partial(kernel, n, o, v, group, rows), out_shape...  45.9 us

profile of v3, /device:TPU:0, one launch (start us, length us, event | category | flops | bytes accessed | tf_op | source)
XLA Modules:
  0.0 46.5 jit_solution(14754467200562353832)
XLA Ops:
  0.0 45.9 %shard_map.55 = f32[4,32]{1,0:T(4,128)S(1)} custom-call(bf16[13,10816,104]{2,1,0:T(8,128)(2,1)} %bitcast.6, bf16[32,104]{1,0:T(8,128)(2,1)} %bitcast.8, bf16[64,104]{1,0:T(8,128)(2,1)} %bitcast.7, f32[32]{0:T(128)} %eo_hbm.1, f32[1,64]{1,0:T(1,128)} %bitcast.9), custom_call_target="tpu_custom_call" | custom-call | tf_op jit(solution)/shard_map/pallas_call | solution.py:249
  45.9 0.6 %copy.7 = f32[32,4]{0,1:T(4,128)} copy(f32[32,4]{0,1:T(4,128)S(1)} %bitcast.5) | data formatting | bytes 1024

commit v4 on v3

--- a/solution.py
+++ b/solution.py
@@ -11,7 +11,8 @@
 MESH = pl.DeviceIdType.MESH
 SUB = 16
 LATE = 5
-FAR, NEAR = (6, 7, 4, 5), (2, 3, 1)
+OPPOSITE, SIDE, NEAR = (6, 7), (4, 5), (2, 3, 1)
+RELAY = 3
 F32 = jnp.float32
 BF16 = jnp.bfloat16
 
@@ -33,9 +34,9 @@
 
 
 def kernel(n, o, v, group, rows, a_hbm, cot_hbm, cvt_hbm, eo_hbm, ev_hbm, e_ref,
-           abuf, cot, cvt, eo, ev_ref, l1, w2, l3, l4, tp, hs, gsend, recv, vacc, rden, esum,
-           a_sem, in_sem, send_sem, recv_sem):
-    me = lax.axis_index("dev")
+           abuf, cot, cvt, eo, ev_ref, l1, w2, l3, l4, tp, hs, gsend, recv, relay, vacc, rden, esum,
+           a_sem, in_sem, send_sem, recv_sem, relay_sem, pass_sem):
+    frag, me = lax.axis_index("frag"), lax.axis_index("dev")
     slots = abuf.shape[0]
     tiles = n // 4
     cuts = [tiles * c // 26 for c in (0, 9, 17, 23, 26)]
@@ -61,6 +62,16 @@
     barrier = pltpu.get_barrier_semaphore()
     for k in range(1, group):
         pl.semaphore_signal(barrier, inc=1, device_id={"dev": peer(k)}, device_id_type=MESH)
+
+    @pl.when(frag == 0)
+    def _():
+        for k in OPPOSITE:
+            pl.semaphore_signal(barrier, inc=1, device_id={"frag": 1, "dev": peer(k)}, device_id_type=MESH)
+
+    @pl.when(frag == 1)
+    def _():
+        pl.semaphore_signal(barrier, inc=1, device_id={"frag": 0, "dev": me}, device_id_type=MESH)
+
     for copy in small:
         copy.wait()
 
@@ -90,6 +101,26 @@
             device_id_type=MESH,
         )
 
+    def aside(k):
+        return pltpu.make_async_remote_copy(
+            src_ref=gsend.at[RELAY, pl.ds(pl.multiple_of((2 * peer(k) + 1) * v, v), v)],
+            dst_ref=relay.at[k % 2],
+            send_sem=send_sem,
+            recv_sem=relay_sem.at[k % 2],
+            device_id={"frag": 1, "dev": me},
+            device_id_type=MESH,
+        )
+
+    def onward(k):
+        return pltpu.make_async_remote_copy(
+            src_ref=relay.at[k % 2],
+            dst_ref=recv.at[1, RELAY, me],
+            send_sem=pass_sem.at[k % 2],
+            recv_sem=recv_sem.at[1, RELAY],
+            device_id={"frag": 0, "dev": peer(k)},
+            device_id_type=MESH,
+        )
+
     pad = jnp.zeros((2 * n, 128 - n), BF16)
 
     def tile(slot, t):
@@ -129,7 +160,7 @@
         hs[at, :] = dot(tp[at, :], w2[...]).astype(BF16)
     load(slots, 0).start()
     finish(0, peer(6) // 2, 1)
-    pl.semaphore_wait(barrier, group - 1)
+    pl.semaphore_wait(barrier, group + frag)
     hand_out(0, (6, 7), (0, 1))
     finish(0, peer(4) // 2, 1)
     hand_out(0, (4, 5), (0, 1))
@@ -149,17 +180,34 @@
 
         hs[...] = dot(tp[...], w2[...]).astype(BF16)
         gsend[p] = dot(l3[...], hs[...]).astype(BF16)
-        hand_out(p, FAR + NEAR, (0,))
+        hand_out(p, OPPOSITE + SIDE + NEAR, (0,))
 
         @pl.when(p < rows - LATE)
         def _():
-            hand_out(p, FAR + NEAR, (1,))
+            detour = (p == RELAY) & (frag == 0)
+
+            @pl.when(detour)
+            def _():
+                for k in OPPOSITE:
+                    aside(k).start()
+
+            @pl.when(jnp.logical_not(detour))
+            def _():
+                hand_out(p, OPPOSITE, (1,))
+
+            hand_out(p, SIDE + NEAR, (1,))
+
+        @pl.when((p == RELAY + 3) & (frag == 1))
+        def _():
+            for k in OPPOSITE:
+                aside(k).wait_recv()
+                onward(k).start()
 
         keep(p)
 
     @pl.loop(rows - LATE, rows)
     def _(p):
-        hand_out(p, FAR + NEAR, (1,))
+        hand_out(p, OPPOSITE + SIDE + NEAR, (1,))
 
     lane = iota((n, SUB * n), 1) // SUB
     spread = ones_where(lane % group * rows + lane // group == iota((n, SUB * n), 0))
@@ -210,24 +258,21 @@
                 mats += [vacc[x, g // 2, at, g % 2 * 128:(g % 2 + 1) * 128] for g in range(v // SUB)]
             mat = jnp.concatenate(mats, axis=0)
             mat_t = jnp.transpose(mat)
-            turned = pltpu.roll(jnp.concatenate([mat_t[v:], mat_t[:v]], axis=0), v, 1)
-            swap = jnp.where(first == even, mat_t, turned)
+            left, right = mat_t[:v], mat_t[v:]
+            turned = pltpu.roll(jnp.where(even[:v], right, left), v, 1)
+            swap = jnp.concatenate([jnp.where(even[:v], left, turned), jnp.where(even[:v], turned, right)], axis=0)
             term = mat * (2.0 * mat - swap) * rden[x, i]
             for i2 in range(2):
                 esum[x, 2 * i + i2] = jnp.sum(term[i2 * v:(i2 + 1) * v].reshape(v // 8, 8, 128), axis=0)
 
-    lane = iota((o, 128), 1)
-    out = jnp.zeros((o, 128), F32)
     for x in range(2):
         add(x, 0, 8)
         add(x, 8, 12)
         add(x, 12, rows)
         energies(x)
-        both = jnp.sum(esum[x], axis=1)
+        both = jnp.transpose(jnp.sum(esum[x], axis=1))
         for jh in range(2):
-            total = jnp.sum(jnp.where(lane // v == jh, both, 0.0), axis=1, keepdims=True)
-            out = jnp.where(lane == 2 * x + jh, total, out)
-    e_ref[...] = jnp.transpose(out)[:o // group, :]
+            e_ref[pl.ds(2 * x + jh, 1), :] = jnp.sum(both[jh * v:(jh + 1) * v], axis=0, keepdims=True)
 
     pltpu.make_async_remote_copy(
         src_ref=gsend.at[:, pl.ds(0, (group - 1) * 2 * v)],
@@ -237,6 +282,11 @@
         device_id={"dev": peer(1)},
         device_id_type=MESH,
     ).wait_send()
+
+    @pl.when(frag == 1)
+    def _():
+        for k in OPPOSITE:
+            onward(k).wait_send()
 
 
 def solution(mesh):
@@ -265,6 +315,7 @@
                 pltpu.VMEM((SUB * n, 128), BF16),
                 pltpu.VMEM((rows, SUB * v, 128), BF16),
                 pltpu.VMEM((2, rows, group, v, 128), BF16),
+                pltpu.VMEM((2, v, 128), BF16),
                 pltpu.VMEM((2, 2, SUB * o, 256), F32),
                 pltpu.VMEM((2, o // 2, 128, 128), F32),
                 pltpu.VMEM((2, o, 8, 128), F32),
@@ -272,6 +323,8 @@
                 pltpu.SemaphoreType.DMA((8,)),
                 pltpu.SemaphoreType.DMA,
                 pltpu.SemaphoreType.DMA((2, rows)),
+                pltpu.SemaphoreType.DMA((2,)),
+                pltpu.SemaphoreType.DMA((2,)),
             ],
             compiler_params=pltpu.CompilerParams(
                 collective_id=0, has_side_effects=True, vmem_limit_bytes=40 * 2**20),

time: 46.7 us -> 45.8 us (0.981)
  Pallas kernels: 45.9 us -> 45 us
    pallas_call x1, Pallas kernels: 45.9 us -> 45 us  [per_device(): pl.pallas_call(functools.partial(kernel, n, o, v, group, rows), out_shape...]
where the time goes in v4:
time: 45.8 us; the launch traced here: 45.6 us
  Pallas kernels  45 us (98%)
  local copies, waits for them, and re-layouts  0.58 us (1%)
    pallas_call x1, Pallas kernels, per_device(): pl.pallas_call(functools.partial(kernel, n, o, v, group, rows), out_shape...  45 us

profile of v4, /device:TPU:0, one launch (start us, length us, event | category | flops | bytes accessed | tf_op | source)
XLA Modules:
  0.0 45.6 jit_solution(1608661342812517049)
XLA Ops:
  0.0 45.0 %shard_map.55 = f32[4,32]{1,0:T(4,128)S(1)} custom-call(bf16[13,10816,104]{2,1,0:T(8,128)(2,1)} %bitcast.6, bf16[32,104]{1,0:T(8,128)(2,1)} %bitcast.8, bf16[64,104]{1,0:T(8,128)(2,1)} %bitcast.7, f32[32]{0:T(128)} %eo_hbm.1, f32[1,64]{1,0:T(1,128)} %bitcast.9), custom_call_target="tpu_custom_call" | custom-call | tf_op jit(solution)/shard_map/pallas_call | solution.py:299
  45.0 0.6 %copy.7 = f32[32,4]{0,1:T(4,128)} copy(f32[32,4]{0,1:T(4,128)S(1)} %bitcast.5) | data formatting | bytes 1024

commit v5 on v4

--- a/solution.py
+++ b/solution.py
@@ -39,7 +39,7 @@
     frag, me = lax.axis_index("frag"), lax.axis_index("dev")
     slots = abuf.shape[0]
     tiles = n // 4
-    cuts = [tiles * c // 26 for c in (0, 9, 17, 23, 26)]
+    cuts = [tiles * c // 26 for c in (0, 16, 26)]
 
     def load(p, slot):
         return pltpu.make_async_copy(a_hbm.at[p], abuf.at[slot], a_sem.at[slot])
@@ -52,7 +52,7 @@
         [(cot_hbm, cot), (cvt_hbm, cvt), (eo_hbm, eo), (ev_hbm, ev_ref)])]
     for copy in small:
         copy.start()
-    for c in range(4):
+    for c in range(2):
         load_first(c).start()
 
     def peer(k):
@@ -76,24 +76,26 @@
         copy.wait()
 
     row = iota((64, o), 0)
-    perm = ones_where(2 * (row % SUB) + row // SUB % 2 == iota((64, o), 1))
+    perm = ones_where(4 * (row % 8) + row // SUB == iota((64, o), 1))
     cotp = dot(perm, cot[...]).astype(BF16)
     spread = ones_where(iota((n, 2 * n), 1) % n == iota((n, 2 * n), 0))
-    same = iota((64, 2 * n), 0) // 32 == iota((64, 2 * n), 1) // n
+    same = iota((64, 2 * n), 0) // 8 % 2 == iota((64, 2 * n), 1) // n
     l1[...] = jnp.where(same, dot(cotp, spread), 0.0).astype(BF16)
     spread = ones_where(iota((256, n), 0) % 128 == iota((256, n), 1))
     same = iota((256, 2 * v), 0) // 128 == iota((256, 2 * v), 1) // v
     cvt2 = jnp.concatenate([cvt[...], cvt[...]], axis=0)
     w2[...] = jnp.where(same, dot_t(spread, cvt2), 0.0).astype(BF16)
-    spread = ones_where(iota((n, SUB * n), 1) // SUB == iota((n, SUB * n), 0))
+    depth = l3.shape[1]
+    spread = ones_where(iota((n, depth), 1) // 8 == iota((n, depth), 0))
     cvrep = dot(cvt[...], spread).astype(BF16)
-    for j in range(SUB):
-        pick = (iota((v, SUB * n), 1) % SUB == j)
+    for j in range(group):
+        pick = iota((v, depth), 1) % 8 == j
         l3[j * v:(j + 1) * v, :] = jnp.where(pick, cvrep, jnp.zeros_like(cvrep))
+    hs[8 * n:, :] = jnp.zeros((depth - 8 * n, 256), BF16)
 
     def send(p, x, k):
         return pltpu.make_async_remote_copy(
-            src_ref=gsend.at[p, pl.ds(pl.multiple_of((2 * peer(k) + x) * v, v), v)],
+            src_ref=gsend.at[p, x, pl.ds(pl.multiple_of(peer(k) * v, v), v)],
             dst_ref=recv.at[x, p, me],
             send_sem=send_sem,
             recv_sem=recv_sem.at[x, p],
@@ -103,7 +105,7 @@
 
     def aside(k):
         return pltpu.make_async_remote_copy(
-            src_ref=gsend.at[RELAY, pl.ds(pl.multiple_of((2 * peer(k) + 1) * v, v), v)],
+            src_ref=gsend.at[RELAY, 1, pl.ds(pl.multiple_of(peer(k) * v, v), v)],
             dst_ref=relay.at[k % 2],
             send_sem=send_sem,
             recv_sem=relay_sem.at[k % 2],
@@ -129,16 +131,19 @@
         right = abuf[slot, pl.ds(base + 2 * n, 2 * n), :]
         out = dot(l1[...], jnp.concatenate([left, pad, right, pad], axis=1)).astype(BF16)
         for qn in range(2):
-            for qk in range(2):
-                to = t * 64 + (2 * qn + qk) * SUB
-                to = pl.ds(to if isinstance(t, int) else pl.multiple_of(to, SUB), SUB)
-                for jh in range(2):
-                    at = qk * 32 + jh * SUB
-                    tp[to, jh * 128:(jh + 1) * 128] = out[at:at + SUB, qn * 128:(qn + 1) * 128]
-
-    def finish(p, chip, chips):
-        at = pl.ds(pl.multiple_of(chip * 4 * v, 4 * v), chips * 4 * v)
-        gsend[p, at, :] = dot(l3[at, :], hs[...]).astype(BF16)
+            to = t * 32 + qn * SUB
+            to = pl.ds(to if isinstance(t, int) else pl.multiple_of(to, SUB), SUB)
+            for jq in range(4):
+                tp[to, jq * 128:(jq + 1) * 128] = out[jq * SUB:(jq + 1) * SUB, qn * 128:(qn + 1) * 128]
+
+    def second(lo, hi):
+        for x in range(2):
+            hs[lo:hi, x * 128:(x + 1) * 128] = dot(tp[lo:hi, x * 256:(x + 1) * 256], w2[...]).astype(BF16)
+
+    def third(p):
+        out = dot(l3[...], hs[...]).astype(BF16)
+        for x in range(2):
+            gsend[p, x] = out[:, x * 128:(x + 1) * 128]
 
     def hand_out(p, ks, xs):
         for x in xs:
@@ -147,25 +152,20 @@
 
     def keep(p):
         for x in range(2):
-            recv[x, p, me] = gsend[p, pl.ds(pl.multiple_of((2 * me + x) * v, v), v), :]
-
-    for c in range(4):
+            recv[x, p, me] = gsend[p, x, pl.ds(pl.multiple_of(me * v, v), v), :]
+
+    for c in range(2):
         load_first(c).wait()
-        if c == 2:
+        if c == 1:
             for p in range(1, slots):
                 load(p, p).start()
         for t in range(cuts[c], cuts[c + 1]):
             tile(0, t)
-        at = slice(cuts[c] * 64, cuts[c + 1] * 64)
-        hs[at, :] = dot(tp[at, :], w2[...]).astype(BF16)
+        second(cuts[c] * 32, cuts[c + 1] * 32)
     load(slots, 0).start()
-    finish(0, peer(6) // 2, 1)
+    third(0)
     pl.semaphore_wait(barrier, group + frag)
-    hand_out(0, (6, 7), (0, 1))
-    finish(0, peer(4) // 2, 1)
-    hand_out(0, (4, 5), (0, 1))
-    finish(0, me // 4 * 2, 2)
-    hand_out(0, NEAR, (0, 1))
+    hand_out(0, OPPOSITE + SIDE + NEAR, (0, 1))
     keep(0)
 
     @pl.loop(1, rows)
@@ -178,8 +178,8 @@
         def _():
             load(p + slots, slot).start()
 
-        hs[...] = dot(tp[...], w2[...]).astype(BF16)
-        gsend[p] = dot(l3[...], hs[...]).astype(BF16)
+        second(0, 8 * n)
+        third(p)
         hand_out(p, OPPOSITE + SIDE + NEAR, (0,))
 
         @pl.when(p < rows - LATE)
@@ -275,8 +275,8 @@
             e_ref[pl.ds(2 * x + jh, 1), :] = jnp.sum(both[jh * v:(jh + 1) * v], axis=0, keepdims=True)
 
     pltpu.make_async_remote_copy(
-        src_ref=gsend.at[:, pl.ds(0, (group - 1) * 2 * v)],
-        dst_ref=gsend.at[:, pl.ds(0, (group - 1) * 2 * v)],
+        src_ref=gsend.at[:, :, pl.ds(0, (group - 1) * v)],
+        dst_ref=gsend.at[:, :, pl.ds(0, (group - 1) * v)],
         send_sem=send_sem,
         recv_sem=recv_sem.at[0, 0],
         device_id={"dev": peer(1)},
@@ -309,11 +309,11 @@
                 pltpu.VMEM((1, v), F32),
                 pltpu.VMEM((64, 2 * n), BF16),
                 pltpu.VMEM((256, 128), BF16),
-                pltpu.VMEM((SUB * v, SUB * n), BF16),
+                pltpu.VMEM((group * v, -(-8 * n // 128) * 128), BF16),
                 pltpu.VMEM((SUB * o, SUB * n), BF16),
-                pltpu.VMEM((SUB * n, 256), BF16),
-                pltpu.VMEM((SUB * n, 128), BF16),
-                pltpu.VMEM((rows, SUB * v, 128), BF16),
+                pltpu.VMEM((8 * n, 512), BF16),
+                pltpu.VMEM((-(-8 * n // 128) * 128, 256), BF16),
+                pltpu.VMEM((rows, 2, group * v, 128), BF16),
                 pltpu.VMEM((2, rows, group, v, 128), BF16),
                 pltpu.VMEM((2, v, 128), BF16),
                 pltpu.VMEM((2, 2, SUB * o, 256), F32),

time: 45.8 us -> 45.1 us (0.985)
  Pallas kernels: 45 us -> 44.3 us
    pallas_call x1, Pallas kernels: 45 us -> 44.3 us  [per_device(): pl.pallas_call(functools.partial(kernel, n, o, v, group, rows), out_shape...]
where the time goes in v5:
time: 45.1 us; the launch traced here: 44.9 us
  Pallas kernels  44.3 us (98%)
  local copies, waits for them, and re-layouts  0.58 us (1%)
    pallas_call x1, Pallas kernels, per_device(): pl.pallas_call(functools.partial(kernel, n, o, v, group, rows), out_shape...  44.3 us

profile of v5, /device:TPU:0, one launch (start us, length us, event | category | flops | bytes accessed | tf_op | source)
XLA Modules:
  0.0 44.9 jit_solution(12219494029976134201)
XLA Ops:
  0.0 44.3 %shard_map.55 = f32[4,32]{1,0:T(4,128)S(1)} custom-call(bf16[13,10816,104]{2,1,0:T(8,128)(2,1)} %bitcast.6, bf16[32,104]{1,0:T(8,128)(2,1)} %bitcast.8, bf16[64,104]{1,0:T(8,128)(2,1)} %bitcast.7, f32[32]{0:T(128)} %eo_hbm.1, f32[1,64]{1,0:T(1,128)} %bitcast.9), custom_call_target="tpu_custom_call" | custom-call | tf_op jit(solution)/shard_map/pallas_call | solution.py:299
  44.3 0.6 %copy.7 = f32[32,4]{0,1:T(4,128)} copy(f32[32,4]{0,1:T(4,128)S(1)} %bitcast.5) | data formatting | bytes 1024

commit v6 on v5

--- a/solution.py
+++ b/solution.py
@@ -39,7 +39,7 @@
     frag, me = lax.axis_index("frag"), lax.axis_index("dev")
     slots = abuf.shape[0]
     tiles = n // 4
-    cuts = [tiles * c // 26 for c in (0, 16, 26)]
+    cuts = [tiles * c // 26 for c in (0, 12, 26)]
 
     def load(p, slot):
         return pltpu.make_async_copy(a_hbm.at[p], abuf.at[slot], a_sem.at[slot])
@@ -207,7 +207,11 @@
 
     @pl.loop(rows - LATE, rows)
     def _(p):
-        hand_out(p, OPPOSITE + SIDE + NEAR, (1,))
+        hand_out(p, OPPOSITE, (1,))
+
+    @pl.loop(rows - LATE, rows)
+    def _(p):
+        hand_out(p, SIDE + NEAR, (1,))
 
     lane = iota((n, SUB * n), 1) // SUB
     spread = ones_where(lane % group * rows + lane // group == iota((n, SUB * n), 0))

time: 45.1 us -> 44.4 us (0.984)
  Pallas kernels: 44.3 us -> 43.6 us
    pallas_call x1, Pallas kernels: 44.3 us -> 43.6 us  [per_device(): pl.pallas_call(functools.partial(kernel, n, o, v, group, rows), out_shape...]
where the time goes in v6:
time: 44.4 us; the launch traced here: 44.2 us
  Pallas kernels  43.6 us (98%)
  local copies, waits for them, and re-layouts  0.58 us (1%)
    pallas_call x1, Pallas kernels, per_device(): pl.pallas_call(functools.partial(kernel, n, o, v, group, rows), out_shape...  43.6 us

profile of v6, /device:TPU:0, one launch (start us, length us, event | category | flops | bytes accessed | tf_op | source)
XLA Modules:
  0.0 44.2 jit_solution(11697036345465627004)
XLA Ops:
  0.0 43.6 %shard_map.55 = f32[4,32]{1,0:T(4,128)S(1)} custom-call(bf16[13,10816,104]{2,1,0:T(8,128)(2,1)} %bitcast.6, bf16[32,104]{1,0:T(8,128)(2,1)} %bitcast.8, bf16[64,104]{1,0:T(8,128)(2,1)} %bitcast.7, f32[32]{0:T(128)} %eo_hbm.1, f32[1,64]{1,0:T(1,128)} %bitcast.9), custom_call_target="tpu_custom_call" | custom-call | tf_op jit(solution)/shard_map/pallas_call | solution.py:303
  43.6 0.6 %copy.7 = f32[32,4]{0,1:T(4,128)} copy(f32[32,4]{0,1:T(4,128)S(1)} %bitcast.5) | data formatting | bytes 1024
